TPU v7x, 32 devices: a whole 2x2x4 slice. The times are simulated.
32 devices in a mesh: grp: 2 (over x), leaf: 16 (over z, y, core).
Axes of the slice: x: 2, y: 2, z: 4, core: 2. Of those that a mesh axis runs over, the one named last changes fastest.
Arguments:
- points: float32 [8, 32768], P(None, ('grp', 'leaf')), may hold values from -6 to 6
- rhs: float32 [16, 32768], P(None, ('grp', 'leaf')), may hold values from -6 to 6
- basis: float32 [32768, 128], P(('grp', 'leaf')), may hold values from -0.1875 to 0.1875
- transfer: float32 [32, 128, 128], P(('grp', 'leaf')), may hold values from -0.5 to 0.5
- noise: float32 [32768], P(('grp', 'leaf')), may hold values from 0.5 to 2
- inv_scale: float32 [8], replicated, may hold values from 0.15 to 0.6
- links: int32 [32, 2], P(('grp', 'leaf')), may hold values from 0 to 1, as said below
- leaf_skel: int32 [32, 128], P(('grp', 'leaf')), may hold values from 0 to 1023, as said below
- group_skel: int32 [2, 128], P('grp'), may hold values from 0 to 2047, as said below
Outputs:
- solution: float32 [16, 32768], P(None, ('grp', 'leaf'))
- residual: float32 [16, 32768], P(None, ('grp', 'leaf'))
Inputs may be any that keep to these rules, and one draw needn't show every extreme that they name: `links`: column 1 of box l equals column 0 of box l + 1; column 0 is 0 for the first box of each group of 16 and column 1 for the last. `leaf_skel`: the 128 indices of a box are distinct. `group_skel`: the 128 indices of a group are distinct.
All inputs are finite; a program needn't handle non-finite values.
Results may differ from a plain program's by a relative error of at most 0.0003.
Values sent between devices are 32-bit elements; how exact they have to be, the bound alone decides.
No kernel may reach another device: no remote copies, remote signals or barrier semaphores. Data moves between devices by JAX's collectives and lax.ppermute only.
A program may use at most 128 MiB of HBM per device.

v0:
```python
import jax
import jax.numpy as jnp
from jax import lax
from jax.sharding import PartitionSpec as P

ITERS = 2


def padded_2(value, sides, width):
    for axis, dim in sides:
        size, length = (lax.axis_size(axis), value.shape[dim])
        up = [(i, (i + 1) % size) for i in range(size - 1)]
        down = [(j, i) for i, j in up]
        last = lax.slice_in_dim(value, length - width, length, axis=dim)
        initial = lax.slice_in_dim(value, 0, width, axis=dim)
        before = lax.ppermute(last, axis, up)
        after = lax.ppermute(initial, axis, down)
        value = jnp.concatenate([before, value, after], axis=dim)
    return value


def kernel_block(left, right, inv_scale):
    first = left * inv_scale[:, None]
    second = right * inv_scale[:, None]
    cross = lax.dot_general(
        first, second, (((0,), (0,)), ((), ())), precision=lax.Precision.HIGHEST
    )
    dist = (
        jnp.sum(first * first, axis=0)[:, None]
        + jnp.sum(second * second, axis=0)[None, :]
        - 2.0 * cross
    )
    scaled = jnp.sqrt(5.0 * jnp.maximum(dist, 0.0))
    return (1.0 + scaled + scaled * scaled / 3.0) * jnp.exp(-scaled)


def contract(first, second):
    return lax.dot_general(first, second, (((1,), (1,)), ((), ())), precision=lax.Precision.HIGHEST)


def product(first, second):
    return jnp.dot(first, second, precision=lax.Precision.HIGHEST)


def two_products(residual, image):
    return lax.psum(
        (jnp.sum(residual * residual, axis=1), jnp.sum(residual * image, axis=1)), ("grp", "leaf")
    )


def local(points, rhs, basis, transfer, noise, inv_scale, links, leaf_skel, group_skel):
    width = points.shape[1]
    left_bit = links[0, 0]
    right_bit = links[0, 1]
    weight_self = 1.0 + (left_bit + right_bit).astype(jnp.float32)
    skel_pts = points[:, leaf_skel[0]]
    group_pts = lax.all_gather(skel_pts, "leaf", axis=1, tiled=True)
    top_pts = group_pts[:, group_skel[0]]
    top_all = lax.all_gather(top_pts, "grp", axis=1, tiled=True)
    kernel_top = kernel_block(top_pts, top_all, inv_scale)
    kernel_far = kernel_block(skel_pts, group_pts, inv_scale)
    kernel_self = kernel_block(points, points, inv_scale)
    square_zero = jnp.zeros((width, width), jnp.float32)
    lift = transfer[0]
    beside_all = padded_2(points, (("leaf", 1),), width)
    kernel_left = lax.cond(
        left_bit > 0,
        lambda: kernel_block(beside_all[:, :width], points, inv_scale),
        lambda: square_zero,
    )
    kernel_right = lax.cond(
        right_bit > 0,
        lambda: kernel_block(beside_all[:, 2 * width :], points, inv_scale),
        lambda: square_zero,
    )

    def near_part(vec):
        padded = padded_2(vec, (("leaf", 1),), width)
        result = weight_self * product(vec, kernel_self)
        result = result + product(padded[:, :width], kernel_left)
        return result + product(padded[:, 2 * width :], kernel_right)

    def apply(vec):
        coeff = product(vec, basis)
        far = contract(lax.all_gather(coeff, "leaf", axis=1, tiled=True), kernel_far)
        group_coeff = lax.psum(product(coeff, lift), "leaf")
        top_coeff = lax.all_gather(group_coeff, "grp", axis=1, tiled=True)
        top = contract(top_coeff, kernel_top)
        row = far + contract(top, lift)
        return noise[None, :] * vec + near_part(vec) + contract(row, basis)

    solution = jnp.zeros_like(rhs)
    residual = rhs
    image = apply(residual)
    norm_now, curve = two_products(residual, image)
    alpha = norm_now / curve
    direction, along = (residual, image)
    for step in range(ITERS):
        solution = solution + alpha[:, None] * direction
        residual = residual - alpha[:, None] * along
        if step + 1 < ITERS:
            image = apply(residual)
            norm_next, curve = two_products(residual, image)
            ratio = norm_next / norm_now
            alpha = norm_next / (curve - ratio * norm_next / alpha)
            direction = residual + ratio[:, None] * direction
            along = image + ratio[:, None] * along
            norm_now = norm_next
    return (solution, residual)


def solution(mesh):
    return jax.shard_map(
        local,
        mesh=mesh,
        in_specs=(
            P(None, ("grp", "leaf")),
            P(None, ("grp", "leaf")),
            P(("grp", "leaf"), None),
            P(("grp", "leaf"), None, None),
            P(("grp", "leaf")),
            P(),
            P(("grp", "leaf"), None),
            P(("grp", "leaf"), None),
            P("grp", None),
        ),
        out_specs=(P(None, ("grp", "leaf")), P(None, ("grp", "leaf"))),
        check_vma=False,
    )
```

profile of v0, /device:TPU:10, one launch (start us, length us, event | category | flops | bytes accessed | tf_op | source)
XLA Modules:
  0.0 289.5 jit_solution(12969170760022450725)
XLA Ops:
  0.6 2.9 collective-permute-start.2
  3.5 1.9 collective-permute-start
  5.5 4.5 %collective-permute-start.3 = (f32[16,1024]{1,0:T(8,128)}, f32[16,1024]{1,0:T(8,128)S(1)}, u32[]{:S(2)}, u32[]{:S(2)}) collective-permute-start(f32[16,1024]{1,0:T(8,128)} %param.14), channel_id=1, source_target_pairs={{1,0},{2,1},{3,2},{4,3},{5,4},{6,5},{7,6},{8,7},{9,8},{10,9},{11,1... | collective-permute-start | bytes 196616 | tf_op jit(solution)/shard_map/ppermute | solution.py:17
  10.0 1.9 collective-permute-start.1
  14.2 1.3 fusion.39
  17.7 1.2 fusion.41
  18.9 17.5 %all_gather.18 = f32[16,2048]{1,0:T(8,128)S(1)} all-gather(f32[16,128]{1,0:T(8,128)S(1)} %fusion.41), channel_id=1, replica_groups=mesh['grp'=2,'leaf'=16] {'leaf'}, dimensions={1}, use_global_device_ids=true | all-gather | bytes 139264 | tf_op jit(solution)/shard_map/all_gather | solution.py:85
  36.4 1.0 fusion.26
  37.4 25.1 %psum.43 = f32[16,128]{1,0:T(8,128)S(1)} all-reduce(f32[16,128]{1,0:T(8,128)S(1)} %fusion.26), channel_id=1, replica_groups=mesh['grp'=2,'leaf'=16] {'leaf'}, use_global_device_ids=true, to_apply=%region_13.14 | all-reduce | flops 2048 | bytes 16384 | tf_op jit(solution)/shard_map/psum | solution.py:86
  62.5 4.4 %all_gather.20 = f32[16,256]{1,0:T(8,128)S(1)} all-gather(f32[16,128]{1,0:T(8,128)S(1)} %psum.43), channel_id=1, replica_groups=mesh['grp'=2,'leaf'=16] {'grp'}, dimensions={1}, use_global_device_ids=true | all-gather | bytes 24576 | tf_op jit(solution)/shard_map/all_gather | solution.py:87
  67.5 25.8 %all-gather = f32[8,2048]{0,1:T(8,128)S(1)} all-gather(f32[8,128]{0,1:T(8,128)S(1)} %bitcast.71), channel_id=2, replica_groups=mesh['grp'=2,'leaf'=16] {'leaf'}, dimensions={1}, use_global_device_ids=true | all-gather | bytes 69632 | tf_op jit(solution)/shard_map/all_gather | solution.py:57
  93.2 1.0 multiply_reduce_fusion.4
  95.7 5.0 %all-gather.1 = f32[8,256]{0,1:T(8,128)S(1)} all-gather(f32[8,128]{0,1:T(8,128)S(1)} %bitcast.70), channel_id=3, replica_groups=mesh['grp'=2,'leaf'=16] {'grp'}, dimensions={1}, use_global_device_ids=true | all-gather | bytes 12288 | tf_op jit(solution)/shard_map/all_gather | solution.py:59
  101.5 6.9 %exponential_multiply_fusion.2 = f32[1024,1024]{1,0:T(8,128)S(1)} fusion(f32[1024]{0:T(1024)S(1)} %multiply_reduce_fusion.12, f32[8,1024]{1,0:T(8,128)} %param.13, f32[8]{0:T(128)} %param.18), kind=kOutput, calls=%fused_computation.14 | convolution fusion | flops 112205824 | bytes 4231200 | tf_op jit(solution)/shard_map/dot_general | solution.py:25
  108.4 1.6 exponential_multiply_fusion.3
  111.7 2.3 convolution_multiply_fusion.3
  115.9 2.5 conditional.2
  115.9 2.5 broadcast.88
  118.4 2.5 conditional.3
  118.4 2.5 broadcast.94
  120.9 4.6 %fusion.40 = f32[1024,16]{0,1:T(8,128)S(1)} fusion(f32[1024,1024]{1,0:T(8,128)} %get-tuple-element.49, f32[16,1024]{1,0:T(8,128)S(1)} %collective-permute-done.3), kind=kOutput, calls=%fused_computation.77 | convolution fusion | flops 201326592 | bytes 4325376 | tf_op jit(solution)/shard_map/dot_general | solution.py:42
  125.6 2.4 multiply_reduce_fusion.8
  128.0 49.4 %all-reduce.1 = (f32[16]{0:T(128)S(1)}, f32[16]{0:T(128)S(1)}) all-reduce(f32[16]{0:T(128)S(1)} %get-tuple-element.33, f32[16]{0:T(128)S(1)} %get-tuple-element.32), channel_id=1, replica_groups=mesh['grp'=2,'leaf'=16] {'grp','leaf'}, use_global_device_ids=true, to_apply=%region_1.0 | all-reduce | flops 32 | bytes 256 | tf_op jit(solution)/shard_map/psum | solution.py:46
  177.4 4.3 %convolution_multiply_fusion.2 = f32[16,1024]{1,0:T(8,128)S(1)} fusion(f32[16,1024]{1,0:T(8,128)S(1)} %multiply_subtract_fusion.1, f32[1024,1024]{1,0:T(8,128)} %copy-done.3, f32[]{:T(128)} %bitcast), kind=kOutput, calls=%fused_computation.26 | convolution fusion | flops 201342976 | bytes 4325380 | tf_op jit(solution)/shard_map/dot_general | solution.py:42
  182.1 1.9 collective-permute-start.5
  184.0 2.4 collective-permute-start.4
  186.6 16.7 %all_gather.22 = f32[16,2048]{1,0:T(8,128)S(1)} all-gather(f32[16,128]{1,0:T(8,128)S(1)} %fusion.46), channel_id=1, replica_groups=mesh['grp'=2,'leaf'=16] {'leaf'}, dimensions={1}, use_global_device_ids=true | all-gather | bytes 139264 | tf_op jit(solution)/shard_map/all_gather | solution.py:85
  203.3 25.0 %psum.46 = f32[16,128]{1,0:T(8,128)S(1)} all-reduce(f32[16,128]{1,0:T(8,128)S(1)} %fusion.23), channel_id=1, replica_groups=mesh['grp'=2,'leaf'=16] {'leaf'}, use_global_device_ids=true, to_apply=%region_20.0 | all-reduce | flops 2048 | bytes 16384 | tf_op jit(solution)/shard_map/psum | solution.py:86
  228.3 4.5 %all_gather.23 = f32[16,256]{1,0:T(8,128)S(1)} all-gather(f32[16,128]{1,0:T(8,128)S(1)} %psum.46), channel_id=1, replica_groups=mesh['grp'=2,'leaf'=16] {'grp'}, dimensions={1}, use_global_device_ids=true | all-gather | bytes 24576 | tf_op jit(solution)/shard_map/all_gather | solution.py:87
  234.2 4.3 %fusion.45 = f32[16,1024]{1,0:T(8,128)S(1)} fusion(f32[16,1024]{1,0:T(8,128)S(1)} %collective-permute-done.5, f32[1024,1024]{1,0:T(8,128)} %get-tuple-element.49), kind=kOutput, calls=%fused_computation.82 | convolution fusion | flops 201326592 | bytes 4325376 | tf_op jit(solution)/shard_map/dot_general | solution.py:42
  238.5 2.1 fusion.18
  241.2 47.5 %all-reduce = (f32[16]{0:T(128)S(1)}, f32[16]{0:T(128)S(1)}) all-reduce(f32[16]{0:T(128)S(1)} %get-tuple-element.31, f32[16]{0:T(128)S(1)} %get-tuple-element.30), channel_id=1, replica_groups=mesh['grp'=2,'leaf'=16] {'grp','leaf'}, use_global_device_ids=true, to_apply=%region_19.0 | all-reduce | flops 32 | bytes 256 | tf_op jit(solution)/shard_map/psum | solution.py:46
  (49 shorter events, 11.6 us)
Async XLA Ops:
  0.6 17.1 %copy-start = (f32[1024,128]{1,0:T(8,128)S(1)}, f32[1024,128]{1,0:T(8,128)}, u32[]{:S(2)}) copy-start(f32[1024,128]{1,0:T(8,128)} %param.15) | copy-start | bytes 1572868
  0.6 117.8 %collective-permute-start.2 = (f32[8,1024]{1,0:T(8,128)}, f32[8,1024]{1,0:T(8,128)S(1)}, u32[]{:S(2)}, u32[]{:S(2)}) collective-permute-start(f32[8,1024]{1,0:T(8,128)} %param.13), channel_id=1, source_target_pairs={{1,0},{2,1},{3,2},{4,3},{5,4},{6,5},{7,6},{8,7},{9,8},{10,9},{11,1... | collective-permute-start | bytes 98312 | tf_op jit(solution)/shard_map/ppermute | solution.py:17
  3.5 112.4 %collective-permute-start = (f32[8,1024]{1,0:T(8,128)}, f32[8,1024]{1,0:T(8,128)S(1)}, u32[]{:S(2)}, u32[]{:S(2)}) collective-permute-start(f32[8,1024]{1,0:T(8,128)} %param.13), channel_id=1, source_target_pairs={{0,1},{1,2},{2,3},{3,4},{4,5},{5,6},{6,7},{7,8},{8,9},{9,10},{10,1... | collective-permute-start | bytes 98312 | tf_op jit(solution)/shard_map/ppermute | solution.py:16
  5.5 115.5 %collective-permute-start.3 = (f32[16,1024]{1,0:T(8,128)}, f32[16,1024]{1,0:T(8,128)S(1)}, u32[]{:S(2)}, u32[]{:S(2)}) collective-permute-start(f32[16,1024]{1,0:T(8,128)} %param.14), channel_id=1, source_target_pairs={{1,0},{2,1},{3,2},{4,3},{5,4},{6,5},{7,6},{8,7},{9,8},{10,9},{11,1... | collective-permute-start | bytes 196616 | tf_op jit(solution)/shard_map/ppermute | solution.py:17
  10.0 115.5 %collective-permute-start.1 = (f32[16,1024]{1,0:T(8,128)}, f32[16,1024]{1,0:T(8,128)S(1)}, u32[]{:S(2)}, u32[]{:S(2)}) collective-permute-start(f32[16,1024]{1,0:T(8,128)} %param.14), channel_id=1, source_target_pairs={{0,1},{1,2},{2,3},{3,4},{4,5},{5,6},{6,7},{7,8},{8,9},{9,10},{10,1... | collective-permute-start | bytes 196616 | tf_op jit(solution)/shard_map/ppermute | solution.py:16
  101.5 6.9 %copy-start.8 = (f32[8]{0:T(128)S(1)}, f32[8]{0:T(128)}, u32[]{:S(2)}) copy-start(f32[8]{0:T(128)} %param.18) | copy-start | bytes 100
  108.3 5.7 %copy-start.3 = (f32[1024,1024]{1,0:T(8,128)}, f32[1024,1024]{1,0:T(8,128)S(1)}, u32[]{:S(2)}) copy-start(f32[1024,1024]{1,0:T(8,128)S(1)} %exponential_multiply_fusion.2) | copy-start | bytes 12582916
  108.3 3.1 %copy-start.5 = (f32[1,128,128]{2,1,0:T(8,128)S(1)}, f32[1,128,128]{2,1,0:T(8,128)}, u32[]{:S(2)}) copy-start(f32[1,128,128]{2,1,0:T(8,128)} %param.16) | copy-start | bytes 196612
  108.4 3.4 %copy-start.4 = (f32[16,1024]{1,0:T(8,128)S(1)}, f32[16,1024]{1,0:T(8,128)}, u32[]{:S(2)}) copy-start(f32[16,1024]{1,0:T(8,128)} %param.14) | copy-start | bytes 196612
  110.0 5.9 %copy-start.6 = (f32[8,1024]{1,0:T(8,128)S(1)}, f32[8,1024]{1,0:T(8,128)}, u32[]{:S(2)}) copy-start(f32[8,1024]{1,0:T(8,128)} %param.13) | copy-start | bytes 98308
  120.9 4.6 %copy-start.7 = (f32[1024]{0:T(1024)S(1)}, f32[1024]{0:T(1024)}, u32[]{:S(2)}) copy-start(f32[1024]{0:T(1024)} %param.17) | copy-start | bytes 12292
  120.9 4.6 %copy-start.1 = (f32[1024,1024]{1,0:T(8,128)S(1)}, f32[1024,1024]{1,0:T(8,128)}, u32[]{:S(2)}) copy-start(f32[1024,1024]{1,0:T(8,128)} %get-tuple-element.48) | copy-start | bytes 12582916
  182.1 52.1 %collective-permute-start.5 = (f32[16,1024]{1,0:T(8,128)S(1)}, f32[16,1024]{1,0:T(8,128)S(1)}, u32[]{:S(2)}, u32[]{:S(2)}) collective-permute-start(f32[16,1024]{1,0:T(8,128)S(1)} %multiply_subtract_fusion.1), channel_id=1, source_target_pairs={{1,0},{2,1},{3,2},{4,3},{5,4},{6,5},{7,6},{8,7},{9,8},{10,9},{11,1... | collective-permute-start | bytes 196616 | tf_op jit(solution)/shard_map/ppermute | solution.py:17
  184.0 54.5 %collective-permute-start.4 = (f32[16,1024]{1,0:T(8,128)S(1)}, f32[16,1024]{1,0:T(8,128)S(1)}, u32[]{:S(2)}, u32[]{:S(2)}) collective-permute-start(f32[16,1024]{1,0:T(8,128)S(1)} %multiply_subtract_fusion.1), channel_id=1, source_target_pairs={{0,1},{1,2},{2,3},{3,4},{4,5},{5,6},{6,7},{7,8},{8,9},{9,10},{10,1... | collective-permute-start | bytes 196616 | tf_op jit(solution)/shard_map/ppermute | solution.py:16
  228.3 10.2 %copy-start.2 = (f32[1024,1024]{1,0:T(8,128)S(1)}, f32[1024,1024]{1,0:T(8,128)}, u32[]{:S(2)}) copy-start(f32[1024,1024]{1,0:T(8,128)} %get-tuple-element.48) | copy-start | bytes 12582916
where the time goes:
time: 290 us
  blocking collectives  221 us (76%)
  matrix products  35.3 us (12%)
  starting transfers between devices  15.6 us (5%)
  local copies, waits for them, and re-layouts  8.64 us (3%)
  other arithmetic  5.55 us (2%)
  between operations  3.6 us (1%)
    psum x2, blocking collectives, two_products(): lax.psum((jnp.sum(residual * residual, axis=1), jnp.sum(residual * image,...  96.9 us
    psum x2, blocking collectives, apply(): group_coeff = lax.psum(product(coeff, lift), 'leaf')  50.1 us
    all_gather x2, blocking collectives, apply(): lax.all_gather(coeff, 'leaf', axis=1, tiled=True)  34.1 us
    all_gather x1, blocking collectives, local(): group_pts = lax.all_gather(skel_pts, 'leaf', axis=1, tiled=True)  25.8 us
    dot_general x10, matrix products, product(): return jnp.dot(first, second, precision=lax.Precision.HIGHEST)  22.7 us
    ppermute x3, starting transfers between devices, padded_2(): after = lax.ppermute(initial, axis, down)  9.35 us
    all_gather x2, blocking collectives, apply(): top_coeff = lax.all_gather(group_coeff, 'grp', axis=1, tiled=True)  8.85 us
    dot_general x3, matrix products, kernel_block(): lax.dot_general(first, second, (((0,), (0,)), ((), ())), precision=lax.Pr...  8.84 us
  transfers between devices with their start and end apart: 6, of which 0 were waited for; matrix products, arithmetic and copies ran while one was open for 13% of the time, Pallas kernels for 0%

commit v1 on v0

--- a/solution.py
+++ b/solution.py
@@ -54,7 +54,8 @@
     right_bit = links[0, 1]
     weight_self = 1.0 + (left_bit + right_bit).astype(jnp.float32)
     skel_pts = points[:, leaf_skel[0]]
-    group_pts = lax.all_gather(skel_pts, "leaf", axis=1, tiled=True)
+    shards = lax.all_gather(skel_pts, "leaf")
+    group_pts = jnp.concatenate(shards, axis=1)
     top_pts = group_pts[:, group_skel[0]]
     top_all = lax.all_gather(top_pts, "grp", axis=1, tiled=True)
     kernel_top = kernel_block(top_pts, top_all, inv_scale)

time: 290 us -> 288 us (level)
  blocking collectives: 221 us -> 218 us
    all_gather x1, blocking collectives: 25.8 us -> 22.6 us  [local(): shards = lax.all_gather(skel_pts, 'leaf')]
  transfers between devices with their start and end apart: 6 -> 6, of which waited for: 0 -> 0; matrix products, arithmetic and copies ran while one was open for 13% -> 14% of each run, Pallas kernels for 0% -> 0%
where the time goes in v1:
time: 288 us; the launch traced here: 287 us
  blocking collectives  218 us (76%)
  matrix products  35.3 us (12%)
  starting transfers between devices  15.6 us (5%)
  local copies, waits for them, and re-layouts  9.02 us (3%)
  other arithmetic  5.3 us (2%)
  between operations  3.61 us (1%)
    psum x2, blocking collectives, two_products(): lax.psum((jnp.sum(residual * residual, axis=1), jnp.sum(residual * image,...  97.2 us
    psum x2, blocking collectives, apply(): group_coeff = lax.psum(product(coeff, lift), 'leaf')  50.1 us
    all_gather x2, blocking collectives, apply(): lax.all_gather(coeff, 'leaf', axis=1, tiled=True)  34 us
    dot_general x10, matrix products, product(): return jnp.dot(first, second, precision=lax.Precision.HIGHEST)  22.7 us
    all_gather x1, blocking collectives, local(): shards = lax.all_gather(skel_pts, 'leaf')  22.6 us
    ppermute x3, starting transfers between devices, padded_2(): after = lax.ppermute(initial, axis, down)  9.35 us
    all_gather x2, blocking collectives, apply(): top_coeff = lax.all_gather(group_coeff, 'grp', axis=1, tiled=True)  8.85 us
    dot_general x3, matrix products, kernel_block(): lax.dot_general(first, second, (((0,), (0,)), ((), ())), precision=lax.Pr...  8.85 us
  transfers between devices with their start and end apart: 6, of which 0 were waited for; matrix products, arithmetic and copies ran while one was open for 14% of the time, Pallas kernels for 0%

profile of v1, /device:TPU:10, one launch (start us, length us, event | category | flops | bytes accessed | tf_op | source)
XLA Modules:
  0.0 286.6 jit_solution(1450332741347102196)
XLA Ops:
  0.6 2.9 %collective-permute-start.2 = (f32[8,1024]{1,0:T(8,128)}, f32[8,1024]{1,0:T(8,128)S(1)}, u32[]{:S(2)}, u32[]{:S(2)}) collective-permute-start(f32[8,1024]{1,0:T(8,128)} %param.13), channel_id=1, source_target_pairs={{1,0},{2,1},{3,2},{4,3},{5,4},{6,5},{7,6},{8,7},{9,8},{10,9},{11,1... | collective-permute-start | bytes 98312 | tf_op jit(solution)/shard_map/ppermute | solution.py:17
  3.5 1.9 collective-permute-start
  5.5 4.5 %collective-permute-start.3 = (f32[16,1024]{1,0:T(8,128)}, f32[16,1024]{1,0:T(8,128)S(1)}, u32[]{:S(2)}, u32[]{:S(2)}) collective-permute-start(f32[16,1024]{1,0:T(8,128)} %param.14), channel_id=1, source_target_pairs={{1,0},{2,1},{3,2},{4,3},{5,4},{6,5},{7,6},{8,7},{9,8},{10,9},{11,1... | collective-permute-start | bytes 196616 | tf_op jit(solution)/shard_map/ppermute | solution.py:17
  10.0 1.9 collective-permute-start.1
  14.2 1.3 fusion.39
  17.7 1.2 fusion.41
  18.9 17.5 %all_gather.21 = f32[16,2048]{1,0:T(8,128)S(1)} all-gather(f32[16,128]{1,0:T(8,128)S(1)} %fusion.41), channel_id=1, replica_groups=mesh['grp'=2,'leaf'=16] {'leaf'}, dimensions={1}, use_global_device_ids=true | all-gather | bytes 139264 | tf_op jit(solution)/shard_map/all_gather | solution.py:86
  36.4 1.0 fusion.26
  37.4 25.1 %psum.43 = f32[16,128]{1,0:T(8,128)S(1)} all-reduce(f32[16,128]{1,0:T(8,128)S(1)} %fusion.26), channel_id=1, replica_groups=mesh['grp'=2,'leaf'=16] {'leaf'}, use_global_device_ids=true, to_apply=%region_13.14 | all-reduce | flops 2048 | bytes 16384 | tf_op jit(solution)/shard_map/psum | solution.py:87
  62.5 4.4 %all_gather.24 = f32[16,256]{1,0:T(8,128)S(1)} all-gather(f32[16,128]{1,0:T(8,128)S(1)} %psum.43), channel_id=1, replica_groups=mesh['grp'=2,'leaf'=16] {'grp'}, dimensions={1}, use_global_device_ids=true | all-gather | bytes 24576 | tf_op jit(solution)/shard_map/all_gather | solution.py:88
  67.5 22.6 %all-gather = f32[128,128]{1,0:T(8,128)S(1)} all-gather(f32[8,128]{1,0:T(8,128)S(1)} %copy.17), channel_id=2, replica_groups=mesh['grp'=2,'leaf'=16] {'leaf'}, dimensions={0}, use_global_device_ids=true | all-gather | bytes 69632 | tf_op jit(solution)/shard_map/all_gather | solution.py:57
  92.6 5.0 %all-gather.1 = f32[8,256]{0,1:T(8,128)S(1)} all-gather(f32[8,128]{0,1:T(8,128)S(1)} %bitcast.79), channel_id=3, replica_groups=mesh['grp'=2,'leaf'=16] {'grp'}, dimensions={1}, use_global_device_ids=true | all-gather | bytes 12288 | tf_op jit(solution)/shard_map/all_gather | solution.py:60
  98.4 6.9 %exponential_multiply_fusion.2 = f32[1024,1024]{1,0:T(8,128)S(1)} fusion(f32[1024]{0:T(1024)S(1)} %multiply_reduce_fusion.12, f32[8,1024]{1,0:T(8,128)} %param.13, f32[8]{0:T(128)} %param.18), kind=kOutput, calls=%fused_computation.14 | convolution fusion | flops 112205824 | bytes 4231200 | tf_op jit(solution)/shard_map/dot_general | solution.py:25
  105.3 1.6 exponential_multiply_fusion.3
  108.7 2.3 convolution_multiply_fusion.3
  112.9 2.5 conditional.2
  112.9 2.5 broadcast.92
  115.4 2.5 conditional.3
  115.4 2.5 broadcast.98
  117.9 4.6 %fusion.40 = f32[1024,16]{0,1:T(8,128)S(1)} fusion(f32[1024,1024]{1,0:T(8,128)} %get-tuple-element.49, f32[16,1024]{1,0:T(8,128)S(1)} %collective-permute-done.3), kind=kOutput, calls=%fused_computation.77 | convolution fusion | flops 201326592 | bytes 4325376 | tf_op jit(solution)/shard_map/dot_general | solution.py:42
  122.5 2.4 multiply_reduce_fusion.7
  124.9 50.2 %all-reduce.1 = (f32[16]{0:T(128)S(1)}, f32[16]{0:T(128)S(1)}) all-reduce(f32[16]{0:T(128)S(1)} %get-tuple-element.33, f32[16]{0:T(128)S(1)} %get-tuple-element.32), channel_id=1, replica_groups=mesh['grp'=2,'leaf'=16] {'grp','leaf'}, use_global_device_ids=true, to_apply=%region_1.0 | all-reduce | flops 32 | bytes 256 | tf_op jit(solution)/shard_map/psum | solution.py:46
  175.2 4.3 %convolution_multiply_fusion.2 = f32[16,1024]{1,0:T(8,128)S(1)} fusion(f32[16,1024]{1,0:T(8,128)S(1)} %multiply_subtract_fusion.1, f32[1024,1024]{1,0:T(8,128)} %copy-done.3, f32[]{:T(128)} %bitcast), kind=kOutput, calls=%fused_computation.26 | convolution fusion | flops 201342976 | bytes 4325380 | tf_op jit(solution)/shard_map/dot_general | solution.py:42
  179.8 1.9 collective-permute-start.5
  181.8 2.4 collective-permute-start.4
  184.3 16.6 %all_gather.26 = f32[16,2048]{1,0:T(8,128)S(1)} all-gather(f32[16,128]{1,0:T(8,128)S(1)} %fusion.46), channel_id=1, replica_groups=mesh['grp'=2,'leaf'=16] {'leaf'}, dimensions={1}, use_global_device_ids=true | all-gather | bytes 139264 | tf_op jit(solution)/shard_map/all_gather | solution.py:86
  200.9 25.0 %psum.46 = f32[16,128]{1,0:T(8,128)S(1)} all-reduce(f32[16,128]{1,0:T(8,128)S(1)} %fusion.23), channel_id=1, replica_groups=mesh['grp'=2,'leaf'=16] {'leaf'}, use_global_device_ids=true, to_apply=%region_20.0 | all-reduce | flops 2048 | bytes 16384 | tf_op jit(solution)/shard_map/psum | solution.py:87
  226.0 4.5 %all_gather.27 = f32[16,256]{1,0:T(8,128)S(1)} all-gather(f32[16,128]{1,0:T(8,128)S(1)} %psum.46), channel_id=1, replica_groups=mesh['grp'=2,'leaf'=16] {'grp'}, dimensions={1}, use_global_device_ids=true | all-gather | bytes 24576 | tf_op jit(solution)/shard_map/all_gather | solution.py:88
  230.6 1.0 fusion.47
  231.9 4.3 %fusion.45 = f32[16,1024]{1,0:T(8,128)S(1)} fusion(f32[16,1024]{1,0:T(8,128)S(1)} %collective-permute-done.5, f32[1024,1024]{1,0:T(8,128)} %get-tuple-element.49), kind=kOutput, calls=%fused_computation.82 | convolution fusion | flops 201326592 | bytes 4325376 | tf_op jit(solution)/shard_map/dot_general | solution.py:42
  236.1 2.1 fusion.18
  238.9 47.0 %all-reduce = (f32[16]{0:T(128)S(1)}, f32[16]{0:T(128)S(1)}) all-reduce(f32[16]{0:T(128)S(1)} %get-tuple-element.31, f32[16]{0:T(128)S(1)} %get-tuple-element.30), channel_id=1, replica_groups=mesh['grp'=2,'leaf'=16] {'grp','leaf'}, use_global_device_ids=true, to_apply=%region_19.0 | all-reduce | flops 32 | bytes 256 | tf_op jit(solution)/shard_map/psum | solution.py:46
  (51 shorter events, 11.7 us)
Async XLA Ops:
  0.6 17.1 %copy-start = (f32[1024,128]{1,0:T(8,128)S(1)}, f32[1024,128]{1,0:T(8,128)}, u32[]{:S(2)}) copy-start(f32[1024,128]{1,0:T(8,128)} %param.15) | copy-start | bytes 1572868
  0.6 114.7 %collective-permute-start.2 = (f32[8,1024]{1,0:T(8,128)}, f32[8,1024]{1,0:T(8,128)S(1)}, u32[]{:S(2)}, u32[]{:S(2)}) collective-permute-start(f32[8,1024]{1,0:T(8,128)} %param.13), channel_id=1, source_target_pairs={{1,0},{2,1},{3,2},{4,3},{5,4},{6,5},{7,6},{8,7},{9,8},{10,9},{11,1... | collective-permute-start | bytes 98312 | tf_op jit(solution)/shard_map/ppermute | solution.py:17
  3.5 109.3 %collective-permute-start = (f32[8,1024]{1,0:T(8,128)}, f32[8,1024]{1,0:T(8,128)S(1)}, u32[]{:S(2)}, u32[]{:S(2)}) collective-permute-start(f32[8,1024]{1,0:T(8,128)} %param.13), channel_id=1, source_target_pairs={{0,1},{1,2},{2,3},{3,4},{4,5},{5,6},{6,7},{7,8},{8,9},{9,10},{10,1... | collective-permute-start | bytes 98312 | tf_op jit(solution)/shard_map/ppermute | solution.py:16
  5.5 112.4 %collective-permute-start.3 = (f32[16,1024]{1,0:T(8,128)}, f32[16,1024]{1,0:T(8,128)S(1)}, u32[]{:S(2)}, u32[]{:S(2)}) collective-permute-start(f32[16,1024]{1,0:T(8,128)} %param.14), channel_id=1, source_target_pairs={{1,0},{2,1},{3,2},{4,3},{5,4},{6,5},{7,6},{8,7},{9,8},{10,9},{11,1... | collective-permute-start | bytes 196616 | tf_op jit(solution)/shard_map/ppermute | solution.py:17
  10.0 112.4 %collective-permute-start.1 = (f32[16,1024]{1,0:T(8,128)}, f32[16,1024]{1,0:T(8,128)S(1)}, u32[]{:S(2)}, u32[]{:S(2)}) collective-permute-start(f32[16,1024]{1,0:T(8,128)} %param.14), channel_id=1, source_target_pairs={{0,1},{1,2},{2,3},{3,4},{4,5},{5,6},{6,7},{7,8},{8,9},{9,10},{10,1... | collective-permute-start | bytes 196616 | tf_op jit(solution)/shard_map/ppermute | solution.py:16
  98.4 6.9 %copy-start.8 = (f32[8]{0:T(128)S(1)}, f32[8]{0:T(128)}, u32[]{:S(2)}) copy-start(f32[8]{0:T(128)} %param.18) | copy-start | bytes 100
  105.3 5.7 %copy-start.3 = (f32[1024,1024]{1,0:T(8,128)}, f32[1024,1024]{1,0:T(8,128)S(1)}, u32[]{:S(2)}) copy-start(f32[1024,1024]{1,0:T(8,128)S(1)} %exponential_multiply_fusion.2) | copy-start | bytes 12582916
  105.3 3.1 %copy-start.5 = (f32[1,128,128]{2,1,0:T(8,128)S(1)}, f32[1,128,128]{2,1,0:T(8,128)}, u32[]{:S(2)}) copy-start(f32[1,128,128]{2,1,0:T(8,128)} %param.16) | copy-start | bytes 196612
  105.3 3.4 %copy-start.4 = (f32[16,1024]{1,0:T(8,128)S(1)}, f32[16,1024]{1,0:T(8,128)}, u32[]{:S(2)}) copy-start(f32[16,1024]{1,0:T(8,128)} %param.14) | copy-start | bytes 196612
  106.9 5.9 %copy-start.6 = (f32[8,1024]{1,0:T(8,128)S(1)}, f32[8,1024]{1,0:T(8,128)}, u32[]{:S(2)}) copy-start(f32[8,1024]{1,0:T(8,128)} %param.13) | copy-start | bytes 98308
  117.9 4.6 %copy-start.7 = (f32[1024]{0:T(1024)S(1)}, f32[1024]{0:T(1024)}, u32[]{:S(2)}) copy-start(f32[1024]{0:T(1024)} %param.17) | copy-start | bytes 12292
  117.9 4.6 %copy-start.1 = (f32[1024,1024]{1,0:T(8,128)S(1)}, f32[1024,1024]{1,0:T(8,128)}, u32[]{:S(2)}) copy-start(f32[1024,1024]{1,0:T(8,128)} %get-tuple-element.48) | copy-start | bytes 12582916
  179.8 52.0 %collective-permute-start.5 = (f32[16,1024]{1,0:T(8,128)S(1)}, f32[16,1024]{1,0:T(8,128)S(1)}, u32[]{:S(2)}, u32[]{:S(2)}) collective-permute-start(f32[16,1024]{1,0:T(8,128)S(1)} %multiply_subtract_fusion.1), channel_id=1, source_target_pairs={{1,0},{2,1},{3,2},{4,3},{5,4},{6,5},{7,6},{8,7},{9,8},{10,9},{11,1... | collective-permute-start | bytes 196616 | tf_op jit(solution)/shard_map/ppermute | solution.py:17
  181.8 54.4 %collective-permute-start.4 = (f32[16,1024]{1,0:T(8,128)S(1)}, f32[16,1024]{1,0:T(8,128)S(1)}, u32[]{:S(2)}, u32[]{:S(2)}) collective-permute-start(f32[16,1024]{1,0:T(8,128)S(1)} %multiply_subtract_fusion.1), channel_id=1, source_target_pairs={{0,1},{1,2},{2,3},{3,4},{4,5},{5,6},{6,7},{7,8},{8,9},{9,10},{10,1... | collective-permute-start | bytes 196616 | tf_op jit(solution)/shard_map/ppermute | solution.py:16
  226.0 10.2 %copy-start.2 = (f32[1024,1024]{1,0:T(8,128)S(1)}, f32[1024,1024]{1,0:T(8,128)}, u32[]{:S(2)}) copy-start(f32[1024,1024]{1,0:T(8,128)} %get-tuple-element.48) | copy-start | bytes 12582916
